TPU v7x, 32 devices: a whole 2x2x4 slice. The times are simulated.
32 devices in a mesh: fsdp: 8 (over z, x), tp: 4 (over y, core).
Axes of the slice: x: 2, y: 2, z: 4, core: 2. Of those that a mesh axis runs over, the one named last changes fastest.
Arguments:
- slopes_in: float32 [32, 128, 4096], P(None, 'fsdp', 'tp'), may hold values from -6 to 6
- moments_in: float32 [32, 128, 4096], P(None, 'fsdp', 'tp'), may hold values from -6 to 6
- weights_in: float32 [32, 128, 4096], P(None, 'fsdp', 'tp'), may hold values from -0.1875 to 0.1875
Outputs:
- new_weights: float32 [32, 128, 4096], P(None, 'fsdp', 'tp')
- new_momentum: float32 [32, 128, 4096], P(None, 'fsdp', 'tp')
All inputs are finite; a program needn't handle non-finite values.
Results may differ from a plain program's by a relative error of at most 0.00021.
Values sent between devices are 32-bit elements; how exact they have to be, the bound alone decides.
A program may use at most 128 MiB of HBM per device.

v0:
```python
import jax
import jax.numpy as jnp
from jax import lax
from jax.sharding import PartitionSpec as P

ITERS = 5
hold_rate = 0.8
learn_rate = 1.0


def body(slopes_in, moments_in, weights_in):
    new_momentum = hold_rate * moments_in + slopes_in
    moved = lax.all_to_all(new_momentum, "fsdp", split_axis=0, concat_axis=1, tiled=True)
    whole = lax.all_to_all(moved, "tp", split_axis=0, concat_axis=2, tiled=True)
    iterate = whole * lax.rsqrt(jnp.sum(whole * whole, axis=(1, 2), keepdims=True) + 1e-06)
    for step in range(ITERS):
        gram = jnp.einsum("mik,mjk->mij", iterate, iterate, precision=lax.Precision.HIGHEST)
        mixed = -4.775 * gram + 2.0315 * jnp.einsum(
            "mij,mjk->mik", gram, gram, precision=lax.Precision.HIGHEST
        )
        iterate = 3.4445 * iterate + jnp.einsum(
            "mij,mjk->mik", mixed, iterate, precision=lax.Precision.HIGHEST
        )
    iterate = lax.all_to_all(iterate, "tp", split_axis=2, concat_axis=0, tiled=True)
    back = lax.all_to_all(iterate, "fsdp", split_axis=1, concat_axis=0, tiled=True)
    new_weights = weights_in - learn_rate * back
    return (new_weights, new_momentum)


def solution(mesh):
    return jax.shard_map(
        body,
        mesh=mesh,
        in_specs=(P(None, "fsdp", "tp"), P(None, "fsdp", "tp"), P(None, "fsdp", "tp")),
        out_specs=(P(None, "fsdp", "tp"), P(None, "fsdp", "tp")),
        check_vma=False,
    )
```

profile of v0, /device:TPU:0, one launch (start us, length us, event | category | flops | bytes accessed | tf_op | source)
XLA Modules:
  0.0 212.4 jit_solution(16108924228545123372)
XLA Ops:
  0.6 2.7 %multiply_add_fusion = f32[32,16,1024]{2,1,0:T(8,128)S(1)} fusion(f32[32,16,1024]{2,1,0:T(8,128)} %param.3, f32[32,16,1024]{2,1,0:T(8,128)} %param.4), kind=kLoop, calls=%fused_computation.11 | loop fusion | flops 1048576 | bytes 6291456 | tf_op jit(solution)/shard_map/add | solution.py:12
  3.3 55.3 %all_to_all.63 = f32[32,16,1024]{2,1,0:T(8,128)S(1)} all-to-all(f32[32,16,1024]{2,1,0:T(8,128)S(1)} %multiply_add_fusion), channel_id=1, replica_groups=mesh['fsdp'=8,'tp'=4] {'fsdp'}, dimensions={0} | all-to-all | bytes 4194304 | tf_op jit(solution)/shard_map/all_to_all | solution.py:13
  58.9 28.3 %all_to_all.64 = f32[4,128,1024]{2,1,0:T(8,128)S(1)} all-to-all(f32[4,128,1024]{2,1,0:T(8,128)S(1)} %bitcast.63), channel_id=1, replica_groups=mesh['fsdp'=8,'tp'=4] {'tp'}, dimensions={0} | all-to-all | bytes 4194304 | tf_op jit(solution)/shard_map/all_to_all | solution.py:14
  88.9 1.8 fusion.4
  91.0 2.6 %multiply_bitcast_fusion.1 = (f32[1,128,4,1024]{3,1,2,0:T(8,128)}, f32[1,128,4,1024]{3,1,2,0:T(8,128)}) fusion(f32[4,128,1024]{2,1,0:T(8,128)S(1)} %all_to_all.64, f32[]{:T(128)S(6)} %rsqrt.4), kind=kLoop, calls=%fused_computation.13 | loop fusion | flops 1048576 | bytes 6291460 | tf_op jit(solution)/shard_map/mul | solution.py:15
  93.5 1.9 copy.32
  95.4 2.9 %copy.31 = f32[1,128,4,1024]{1,3,2,0:T(8,128)} copy(f32[1,128,4,1024]{3,1,2,0:T(8,128)} %get-tuple-element.3) | data formatting | bytes 4194304 | tf_op jit(solution)/shard_map/mul | solution.py:21
  98.3 3.0 %copy.33 = f32[128,4096]{1,0:T(8,128)} copy(f32[128,4096]{0,1:T(8,128)} %bitcast.64) | data formatting | bytes 4194304 | tf_op jit(solution)/shard_map/mul | solution.py:21
  101.3 3.6 %convolution_add_fusion.4 = f32[128,4096]{1,0:T(8,128)S(1)} fusion(f32[128,4096]{1,0:T(8,128)} %copy.33, f32[128,128]{1,0:T(8,128)S(1)} %fusion.11, f32[128,4096]{0,1:T(8,128)S(1)} %bitcast.62), kind=kOutput, calls=%fused_computation.5 | convolution fusion | flops 805830656 | bytes 6356992 | tf_op jit(solution)/shard_map/mij,mjk->mik/dot_general | solution.py:21
  104.9 1.8 fusion.13
  106.9 2.0 convolution_add_fusion.3
  108.9 1.8 fusion.14
  110.9 2.0 convolution_add_fusion.2
  113.0 1.8 fusion.15
  115.0 2.3 %convolution_add_fusion.1 = f32[128,4096]{1,0:T(8,128)S(1)} fusion(f32[128,128]{1,0:T(8,128)S(1)} %fusion.8, f32[128,4096]{1,0:T(8,128)S(1)} %convolution_add_fusion.2), kind=kOutput, calls=%fused_computation.2 | convolution fusion | flops 806354944 | bytes 4259840 | tf_op jit(solution)/shard_map/mij,mjk->mik/dot_general | solution.py:21
  117.3 1.8 fusion.16
  119.3 2.0 fusion
  121.3 3.7 %copy.34 = f32[1,128,4096]{1,0,2:T(1,128)} copy(f32[1,128,4096]{2,1,0:T(8,128)S(1)} %fusion) | data formatting | bytes 4194304 | tf_op jit(solution)/shard_map/add | solution.py:21
  125.0 29.2 %all_to_all.65 = f32[1,128,4096]{1,0,2:T(1,128)S(1)} all-to-all(f32[1,128,4096]{1,0,2:T(1,128)} %copy.34), channel_id=1, replica_groups=mesh['fsdp'=8,'tp'=4] {'tp'}, dimensions={2} | all-to-all | bytes 4194304 | tf_op jit(solution)/shard_map/all_to_all | solution.py:24
  154.3 2.0 copy.35
  156.2 51.7 %all_to_all.66 = f32[4,128,1024]{2,0,1:T(4,128)S(1)} all-to-all(f32[4,128,1024]{2,0,1:T(4,128)} %copy.35), channel_id=1, replica_groups=mesh['fsdp'=8,'tp'=4] {'fsdp'}, dimensions={1} | all-to-all | bytes 4194304 | tf_op jit(solution)/shard_map/all_to_all | solution.py:25
  207.9 1.2 copy.36
  209.4 1.3 copy-done.1
  210.7 1.7 bitcast_subtract_fusion
  (11 shorter events, 2.6 us)
Async XLA Ops:
  3.3 55.3 %copy-start = (f32[32,16,1024]{2,1,0:T(8,128)}, f32[32,16,1024]{2,1,0:T(8,128)S(1)}, u32[]{:S(2)}) copy-start(f32[32,16,1024]{2,1,0:T(8,128)S(1)} %multiply_add_fusion) | copy-start | bytes 6291460
  209.1 1.6 copy-start.1
where the time goes:
time: 213 us; the launch traced here: 212 us
  blocking collectives  164 us (77%)
  matrix products  22 us (10%)
  local copies, waits for them, and re-layouts  16.4 us (8%)
  other arithmetic  8.09 us (4%)
    all_to_all x1, blocking collectives, body(): lax.all_to_all(new_momentum, 'fsdp', split_axis=0, concat_axis=1, tiled=T...  55.3 us
    all_to_all x1, blocking collectives, body(): lax.all_to_all(iterate, 'fsdp', split_axis=1, concat_axis=0, tiled=True)  51.7 us
    all_to_all x1, blocking collectives, body(): lax.all_to_all(iterate, 'tp', split_axis=2, concat_axis=0, tiled=True)  29.2 us
    all_to_all x1, blocking collectives, body(): whole = lax.all_to_all(moved, 'tp', split_axis=0, concat_axis=2, tiled=True)  28.3 us
    dot_general x5, matrix products, body(): jnp.einsum('mij,mjk->mik', mixed, iterate, precision=lax.Precision.HIGHEST)  12 us
    dot_general x5, matrix products, body(): jnp.einsum('mik,mjk->mij', iterate, iterate, precision=lax.Precision.HIGH...  8.96 us
    mul x2, local copies, waits for them, and re-layouts, body(): 3.4445 * iterate  5.84 us

commit v1 on v0

--- a/solution.py
+++ b/solution.py
@@ -21,7 +21,9 @@
         iterate = 3.4445 * iterate + jnp.einsum(
             "mij,mjk->mik", mixed, iterate, precision=lax.Precision.HIGHEST
         )
-    iterate = lax.all_to_all(iterate, "tp", split_axis=2, concat_axis=0, tiled=True)
+    cells = jnp.split(iterate, lax.axis_size("tp"), axis=2)
+    incoming = lax.all_to_all(jnp.stack(cells), "tp", 0, 0)
+    iterate = jnp.concatenate(incoming, axis=0)
     back = lax.all_to_all(iterate, "fsdp", split_axis=1, concat_axis=0, tiled=True)
     new_weights = weights_in - learn_rate * back
     return (new_weights, new_momentum)

time: 213 us -> 206 us (0.967)
  local copies, waits for them, and re-layouts: 16.4 us -> 11.1 us
    add x1 -> x0, local copies, waits for them, and re-layouts: 3.7 us -> none  [body(): 3.4445 * iterate]
where the time goes in v1:
time: 206 us
  blocking collectives  163 us (79%)
  matrix products  22 us (11%)
  local copies, waits for them, and re-layouts  11.1 us (5%)
  other arithmetic  8.32 us (4%)
    all_to_all x1, blocking collectives, body(): lax.all_to_all(new_momentum, 'fsdp', split_axis=0, concat_axis=1, tiled=T...  55.3 us
    all_to_all x1, blocking collectives, body(): lax.all_to_all(iterate, 'fsdp', split_axis=1, concat_axis=0, tiled=True)  51.4 us
    all_to_all x1, blocking collectives, body(): whole = lax.all_to_all(moved, 'tp', split_axis=0, concat_axis=2, tiled=True)  28.3 us
    all_to_all x1, blocking collectives, body(): incoming = lax.all_to_all(jnp.stack(cells), 'tp', 0, 0)  28.1 us
    dot_general x5, matrix products, body(): jnp.einsum('mij,mjk->mik', mixed, iterate, precision=lax.Precision.HIGHEST)  12 us
    dot_general x5, matrix products, body(): jnp.einsum('mik,mjk->mij', iterate, iterate, precision=lax.Precision.HIGH...  8.96 us
    mul x2, local copies, waits for them, and re-layouts, body(): 3.4445 * iterate  5.8 us

profile of v1, /device:TPU:0, one launch (start us, length us, event | category | flops | bytes accessed | tf_op | source)
XLA Modules:
  0.0 206.0 jit_solution(1334329843250225756)
XLA Ops:
  0.6 2.7 %multiply_add_fusion = f32[32,16,1024]{2,1,0:T(8,128)S(1)} fusion(f32[32,16,1024]{2,1,0:T(8,128)} %param.3, f32[32,16,1024]{2,1,0:T(8,128)} %param.4), kind=kLoop, calls=%fused_computation.12 | loop fusion | flops 1048576 | bytes 6291456 | tf_op jit(solution)/shard_map/add | solution.py:12
  3.3 55.3 %all_to_all.50 = f32[32,16,1024]{2,1,0:T(8,128)S(1)} all-to-all(f32[32,16,1024]{2,1,0:T(8,128)S(1)} %multiply_add_fusion), channel_id=1, replica_groups=mesh['fsdp'=8,'tp'=4] {'fsdp'}, dimensions={0} | all-to-all | bytes 4194304 | tf_op jit(solution)/shard_map/all_to_all | solution.py:13
  58.9 28.3 %all_to_all.51 = f32[4,128,1024]{2,1,0:T(8,128)S(1)} all-to-all(f32[4,128,1024]{2,1,0:T(8,128)S(1)} %bitcast.67), channel_id=1, replica_groups=mesh['fsdp'=8,'tp'=4] {'tp'}, dimensions={0} | all-to-all | bytes 4194304 | tf_op jit(solution)/shard_map/all_to_all | solution.py:14
  87.1 1.1 multiply_reduce_fusion
  88.9 1.8 fusion.4
  91.0 2.6 %multiply_bitcast_fusion.1 = (f32[1,128,4,1024]{3,1,2,0:T(8,128)}, f32[1,128,4,1024]{3,1,2,0:T(8,128)}) fusion(f32[4,128,1024]{2,1,0:T(8,128)S(1)} %all_to_all.51, f32[]{:T(128)S(6)} %rsqrt.4), kind=kLoop, calls=%fused_computation.14 | loop fusion | flops 1048576 | bytes 6291460 | tf_op jit(solution)/shard_map/mul | solution.py:15
  93.5 1.9 copy.14
  95.4 2.9 %copy.13 = f32[1,128,4,1024]{1,3,2,0:T(8,128)} copy(f32[1,128,4,1024]{3,1,2,0:T(8,128)} %get-tuple-element.7) | data formatting | bytes 4194304 | tf_op jit(solution)/shard_map/mul | solution.py:21
  98.3 2.9 %copy.15 = f32[128,4096]{1,0:T(8,128)} copy(f32[128,4096]{0,1:T(8,128)} %bitcast.68) | data formatting | bytes 4194304 | tf_op jit(solution)/shard_map/mul | solution.py:21
  101.2 3.6 %convolution_add_fusion.4 = f32[128,4096]{1,0:T(8,128)S(1)} fusion(f32[128,4096]{1,0:T(8,128)} %copy.15, f32[128,128]{1,0:T(8,128)S(1)} %fusion.11, f32[128,4096]{0,1:T(8,128)S(1)} %bitcast.66), kind=kOutput, calls=%fused_computation.5 | convolution fusion | flops 805830656 | bytes 6356992 | tf_op jit(solution)/shard_map/mij,mjk->mik/dot_general | solution.py:21
  104.8 1.8 fusion.13
  106.8 2.0 convolution_add_fusion.3
  108.9 1.8 fusion.14
  110.9 2.0 convolution_add_fusion.2
  112.9 1.8 fusion.15
  114.9 2.3 %convolution_add_fusion.1 = f32[128,4096]{1,0:T(8,128)S(1)} fusion(f32[128,128]{1,0:T(8,128)S(1)} %fusion.8, f32[128,4096]{1,0:T(8,128)S(1)} %convolution_add_fusion.2), kind=kOutput, calls=%fused_computation.2 | convolution fusion | flops 806354944 | bytes 4259840 | tf_op jit(solution)/shard_map/mij,mjk->mik/dot_general | solution.py:21
  117.2 1.8 fusion.16
  119.3 2.0 fusion
  121.8 28.1 %all_to_all.52 = f32[4,1,128,1024]{3,2,1,0:T(8,128)S(1)} all-to-all(f32[4,1,128,1024]{3,2,1,0:T(8,128)S(1)} %pad_maximum_fusion), channel_id=1, replica_groups=mesh['fsdp'=8,'tp'=4] {'tp'}, dimensions={0} | all-to-all | bytes 4194304 | tf_op jit(solution)/shard_map/all_to_all | solution.py:25
  149.9 1.4 copy.16
  151.3 51.4 %all_to_all.53 = f32[4,128,1024]{2,0,1:T(4,128)S(1)} all-to-all(f32[4,128,1024]{2,0,1:T(4,128)S(1)} %copy.16), channel_id=1, replica_groups=mesh['fsdp'=8,'tp'=4] {'fsdp'}, dimensions={1} | all-to-all | bytes 4194304 | tf_op jit(solution)/shard_map/all_to_all | solution.py:27
  202.6 1.2 copy.17
  203.8 0.4 copy-done.1
  204.2 1.7 bitcast_subtract_fusion
  (11 shorter events, 1.8 us)
Async XLA Ops:
  3.3 55.3 %copy-start = (f32[32,16,1024]{2,1,0:T(8,128)}, f32[32,16,1024]{2,1,0:T(8,128)S(1)}, u32[]{:S(2)}) copy-start(f32[32,16,1024]{2,1,0:T(8,128)S(1)} %multiply_add_fusion) | copy-start | bytes 6291460
  202.6 1.6 copy-start.1
